TPU v7x, 32 devices: a whole 2x2x4 slice. The times are simulated.
32 devices in a mesh: gx: 4 (over x, core), gy: 8 (over z, y).
Axes of the slice: x: 2, y: 2, z: 4, core: 2. Of those that a mesh axis runs over, the one named last changes fastest.
Arguments:
- hot_ids: int32 [262144], P(('gx', 'gy')), may hold values from 0 to 2047
- hot_grads: bfloat16 [262144, 128], P(('gx', 'gy')), may hold values from -6 to 6
- cold_grads: bfloat16 [4, 8, 8, 512, 128], P('gx', 'gy'), may hold values from -6 to 6
- cold_slots: int32 [4, 8, 8, 512], P('gx', 'gy'), may hold values from 0 to 2047
- cold_counts: int32 [4, 8, 8], P('gx', 'gy'), may hold values from 1 to 512, as said below
Outputs:
- hot_grad: float32 [2048, 128], replicated
- cold_grad: float32 [4, 16384, 128], P('gx', 'gy')
Inputs may be any that keep to these rules, and one draw needn't show every extreme that they name: In each group g, some owner d receives cold_counts[g, s, d] = 512 from every s; loads per owner are skewed.
All inputs are finite; a program needn't handle non-finite values.
Results may differ from a plain program's by a relative error of at most 0.0003.
Values may be sent and summed in bfloat16 or wider, within the bound.
A program may use at most 64 MiB of HBM per device.

v0:
```python
import math
import jax
import jax.numpy as jnp
from jax import lax
from jax.sharding import PartitionSpec as P

HOT = 2048
OWN_ROWS = 2048


def onehot_sum(row_ids, row_data, table_size, block_rows):
    turns = row_ids.shape[0] // block_rows
    id_blocks = row_ids.reshape(turns, block_rows)
    data_blocks = row_data.reshape(turns, block_rows, row_data.shape[1])
    table_iota = lax.broadcasted_iota(jnp.int32, (table_size, block_rows), 0)

    def add_block(total, pieces):
        ids_here, data_here = pieces
        selector = (table_iota == ids_here[None, :]).astype(jnp.bfloat16)
        return (total + jnp.dot(selector, data_here, preferred_element_type=jnp.float32), None)

    start = jnp.zeros((table_size, row_data.shape[1]), jnp.float32)
    total, unused = lax.scan(add_block, start, (id_blocks, data_blocks))
    return total


def hot_part(hot_ids, hot_grads):
    hot_rows = HOT
    block_rows = math.gcd(hot_ids.shape[0], 2048)
    local_sum = onehot_sum(hot_ids, hot_grads, hot_rows, block_rows)
    factor = (hot_rows / (hot_ids.shape[0] * lax.axis_size("gx") * lax.axis_size("gy"))) ** 0.5
    shared = lax.psum_scatter(local_sum, "gy", scatter_dimension=0, tiled=True)
    shared = lax.psum(shared, "gx")
    total = lax.all_gather(shared, "gy", axis=0, tiled=True)
    return total * factor


def cold_part(cold_grads, cold_slots, cold_counts):
    owners, capacity, width = (cold_grads.shape[2], cold_grads.shape[3], cold_grads.shape[4])
    grads_here = cold_grads.reshape(owners, capacity, width)
    slots_here = cold_slots.reshape(owners, capacity)
    counts_here = cold_counts.reshape(owners)
    places = lax.broadcasted_iota(jnp.int32, (owners, capacity), 1)
    valid = places < counts_here[:, None]
    payload = jnp.where(valid[:, :, None], grads_here, jnp.zeros_like(grads_here))
    got_rows, got_slots = (
        lax.all_to_all(payload, "gy", split_axis=0, concat_axis=0, tiled=True),
        lax.all_to_all(slots_here, "gy", split_axis=0, concat_axis=0, tiled=True),
    )
    total_rows = owners * capacity
    block_rows = math.gcd(total_rows, 1024)
    table = onehot_sum(
        got_slots.reshape(total_rows), got_rows.reshape(total_rows, width), OWN_ROWS, block_rows
    )
    return table.reshape(1, OWN_ROWS, width)


def per_device(hot_ids, hot_grads, cold_grads, cold_slots, cold_counts):
    hot_grad = hot_part(hot_ids, hot_grads)
    cold_grad = cold_part(cold_grads, cold_slots, cold_counts)
    return (hot_grad, cold_grad)


def solution(mesh):
    return jax.shard_map(
        per_device,
        mesh=mesh,
        in_specs=(
            P(("gx", "gy")),
            P(("gx", "gy"), None),
            P("gx", "gy", None, None, None),
            P("gx", "gy", None, None),
            P("gx", "gy", None),
        ),
        out_specs=(P(), P("gx", "gy", None)),
        check_vma=False,
    )
```

profile of v0, /device:TPU:0, one launch (start us, length us, event | category | flops | bytes accessed | tf_op | source)
XLA Modules:
  0.0 185.8 jit_solution(4274179711939193013)
XLA Ops:
  7.2 0.0 reduce-scatter.2.cloned.1.call-start
  7.2 0.8 reshape.43
  8.0 0.0 copy-start.2
  8.0 0.0 copy-start.3
  8.0 0.0 copy-start
  8.0 17.7 %while.22 = (s32[]{:T(128)}, f32[2048,128]{1,0:T(8,128)S(1)}, s32[4,2048]{1,0:T(4,128)S(1)}, bf16[4,2048,128]{2,1,0:T(8,128)(2,1)}, s32[]{:T(128)}, /*index=5*/s32[]{:T(128)}) while((s32[]{:T(128)}, f32[2048,128]{1,0:T(8,128)S(1)}, s32[4,2048]{1,0:T(4,128)S(1)}, bf16[4,2048,128]{2,1,0:T(8,128)(2,1)}, s32[]{:T(128)}, ...), condition=%wide.region_1.2_spmd.clone, body=%wide.region_0.1_spmd.clone.sunk | while | flops 1078460416 | bytes 2646611 | solution.py:23
  8.1 4.4 %fusion.21 = f32[2048,128]{1,0:T(8,128)S(1)} fusion(s32[2048]{0:T(1024)S(1)} %bitcast.25, f32[2048,128]{1,0:T(8,128)S(1)} %get-tuple-element.165, bf16[4,2048,128]{2,1,0:T(8,128)(2,1)} %get-tuple-element.173, s32[]{:T(128)} %get-tuple-element.164, pred[]{:T(512)S(6)} %compare.6), kind=kOutput, calls=%fused_computation.5.clone.1 | convolution fusion | flops 1078460416 | bytes 2630145 | tf_op jit(solution)/shard_map/while/body/eval_jaxpr/dot_general | solution.py:20
  12.6 4.4 %fusion.21 = f32[2048,128]{1,0:T(8,128)S(1)} fusion(s32[2048]{0:T(1024)S(1)} %bitcast.25, f32[2048,128]{1,0:T(8,128)S(1)} %get-tuple-element.165, bf16[4,2048,128]{2,1,0:T(8,128)(2,1)} %get-tuple-element.173, s32[]{:T(128)} %get-tuple-element.164, pred[]{:T(512)S(6)} %compare.6), kind=kOutput, calls=%fused_computation.5.clone.1 | convolution fusion | flops 1078460416 | bytes 2630145 | tf_op jit(solution)/shard_map/while/body/eval_jaxpr/dot_general | solution.py:20
  17.0 4.4 %fusion.21 = f32[2048,128]{1,0:T(8,128)S(1)} fusion(s32[2048]{0:T(1024)S(1)} %bitcast.25, f32[2048,128]{1,0:T(8,128)S(1)} %get-tuple-element.165, bf16[4,2048,128]{2,1,0:T(8,128)(2,1)} %get-tuple-element.173, s32[]{:T(128)} %get-tuple-element.164, pred[]{:T(512)S(6)} %compare.6), kind=kOutput, calls=%fused_computation.5.clone.1 | convolution fusion | flops 1078460416 | bytes 2630145 | tf_op jit(solution)/shard_map/while/body/eval_jaxpr/dot_general | solution.py:20
  21.4 4.4 %fusion.21 = f32[2048,128]{1,0:T(8,128)S(1)} fusion(s32[2048]{0:T(1024)S(1)} %bitcast.25, f32[2048,128]{1,0:T(8,128)S(1)} %get-tuple-element.165, bf16[4,2048,128]{2,1,0:T(8,128)(2,1)} %get-tuple-element.173, s32[]{:T(128)} %get-tuple-element.164, pred[]{:T(512)S(6)} %compare.6), kind=kOutput, calls=%fused_computation.5.clone.1 | convolution fusion | flops 1078460416 | bytes 2630145 | tf_op jit(solution)/shard_map/while/body/eval_jaxpr/dot_general | solution.py:20
  25.7 0.0 copy-start.1
  25.8 1.0 copy-done.1
  26.7 0.0 reduce-scatter.2.cloned.1.call-update
  26.7 0.0 copy-done.2
  26.8 0.6 all_to_all.9
  27.4 7.3 %all-to-all-start = ((s32[8,1,512]{2,1,0:T(1,128)}), s32[8,1,512]{2,1,0:T(1,128)S(1)}, u32[]{:S(2)}, u32[]{:S(2)}) async-start(s32[8,1,512]{2,1,0:T(1,128)} %all_to_all.9), calls=%async_computation.1 | async-start | bytes 32768 | tf_op jit(solution)/shard_map/all_to_all | solution.py:48
  34.7 0.0 copy-done.3
  34.7 0.1 iota_compare_fusion.8
  34.8 0.0 copy-done
  34.8 1.5 bitcast_select_fusion
  36.2 5.1 %all-to-all-done = s32[8,1,512]{2,1,0:T(1,128)S(1)} async-done(((s32[8,1,512]{2,1,0:T(1,128)}), s32[8,1,512]{2,1,0:T(1,128)S(1)}, u32[]{:S(2)}, u32[]{:S(2)}) %all-to-all-start) | async-done | bytes 16416 | tf_op jit(solution)/shard_map/all_to_all | solution.py:48
  41.3 3.6 %all-to-all-start.1 = ((bf16[8,512,128]{2,1,0:T(8,128)(2,1)}), bf16[8,512,128]{2,1,0:T(8,128)(2,1)S(1)}, u32[]{:S(2)}, u32[]{:S(2)}) async-start(bf16[8,512,128]{2,1,0:T(8,128)(2,1)} %bitcast_select_fusion), calls=%async_computation.2 | async-start | bytes 2097152 | tf_op jit(solution)/shard_map/all_to_all | solution.py:47
  44.9 0.0 all-reduce.2.cloned.1.call-start
  44.9 56.6 %reduce-scatter.2.cloned.1.call-done = f32[256,128]{1,0:T(8,128)} async-done(((f32[2048,128]{1,0:T(8,128)}), f32[256,128]{1,0:T(8,128)}) %reduce-scatter.2.cloned.1.call-update) | async-done | bytes 131088 | tf_op jit(solution)/shard_map/reduce_scatter | solution.py:32
  101.6 0.0 all-reduce.2.cloned.1.call-update
  101.6 0.0 all-gather.2.cloned.1.call-start
  101.6 32.9 %all-reduce.2.cloned.1.call-done = f32[256,128]{1,0:T(8,128)} async-done(((f32[256,128]{1,0:T(8,128)}), f32[256,128]{1,0:T(8,128)}) %all-reduce.2.cloned.1.call-update) | async-done | bytes 131088 | tf_op jit(solution)/shard_map/psum | solution.py:33
  134.6 0.0 all-gather.2.cloned.1.call-update
  134.7 0.0 all-to-all-done.1
  134.7 7.3 %while.23 = (s32[]{:T(128)}, f32[2048,128]{1,0:T(8,128)S(1)}, s32[4,1024]{1,0:T(4,128)S(1)}, bf16[4,1024,128]{2,1,0:T(8,128)(2,1)S(1)}, s32[]{:T(128)}, /*index=5*/s32[]{:T(128)}) while((s32[]{:T(128)}, f32[2048,128]{1,0:T(8,128)S(1)}, s32[4,1024]{1,0:T(4,128)S(1)}, bf16[4,1024,128]{2,1,0:T(8,128)(2,1)S(1)}, s32[]{:T(128)}, ...), condition=%wide.region_5.6_spmd.clone, body=%wide.region_4.5_spmd.clone.sunk | while | flops 539492352 | bytes 2371671 | solution.py:23
  134.7 1.8 fusion.23
  136.5 1.8 fusion.23
  138.4 1.8 fusion.23
  140.2 1.8 fusion.23
  142.0 0.0 copy-start.4
  142.0 35.0 %all-gather.2.cloned.1.call-done = f32[2048,128]{1,0:T(8,128)} async-done(((f32[256,128]{1,0:T(8,128)}), f32[2048,128]{1,0:T(8,128)}) %all-gather.2.cloned.1.call-update) | async-done | bytes 1048592 | tf_op jit(solution)/shard_map/all_gather | solution.py:34
  177.0 2.3 %broadcast_multiply_fusion = f32[2048,128]{1,0:T(8,128)} fusion(f32[2048,128]{1,0:T(8,128)} %all-gather.2.cloned.1.call-done), kind=kLoop, calls=%fused_computation.19 | loop fusion | flops 262144 | bytes 2097152 | tf_op jit(solution)/shard_map/mul | solution.py:35
  179.3 0.0 copy-done.4
  (12 shorter events, 0.1 us)
Async XLA Ops:
  7.2 94.4 %reduce-scatter.2.cloned.1.call-start = ((), (), s32[]{:S(2)}) async-start(), calls=%async_computation.3 | async-start | bytes 1179648 | tf_op jit(solution)/shard_map/reduce_scatter | solution.py:32
  8.0 18.8 %copy-start.2 = (s32[1,1,8,512]{3,2,1,0:T(8,128)S(1)}, s32[1,1,8,512]{3,2,1,0:T(8,128)}, u32[]{:S(2)}) copy-start(s32[1,1,8,512]{3,2,1,0:T(8,128)} %param.12) | copy-start | bytes 49156
  8.0 26.7 %copy-start.3 = (s32[1,1,8]{2,1,0:T(1,128)S(1)}, s32[1,1,8]{2,1,0:T(1,128)}, u32[]{:S(2)}) copy-start(s32[1,1,8]{2,1,0:T(1,128)} %param.13) | copy-start | bytes 100
  8.0 26.7 %copy-start = (bf16[1,1,8,512,128]{4,3,2,1,0:T(8,128)(2,1)S(1)}, bf16[1,1,8,512,128]{4,3,2,1,0:T(8,128)(2,1)}, u32[]{:S(2)}) copy-start(bf16[1,1,8,512,128]{4,3,2,1,0:T(8,128)(2,1)} %param.11) | copy-start | bytes 3145732
  25.7 1.0 copy-start.1
  27.4 13.9 %all-to-all-start = ((s32[8,1,512]{2,1,0:T(1,128)}), s32[8,1,512]{2,1,0:T(1,128)S(1)}, u32[]{:S(2)}, u32[]{:S(2)}) async-start(s32[8,1,512]{2,1,0:T(1,128)} %all_to_all.9), calls=%async_computation.1 | async-start | bytes 32768 | tf_op jit(solution)/shard_map/all_to_all | solution.py:48
  41.3 93.4 %all-to-all-start.1 = ((bf16[8,512,128]{2,1,0:T(8,128)(2,1)}), bf16[8,512,128]{2,1,0:T(8,128)(2,1)S(1)}, u32[]{:S(2)}, u32[]{:S(2)}) async-start(bf16[8,512,128]{2,1,0:T(8,128)(2,1)} %bitcast_select_fusion), calls=%async_computation.2 | async-start | bytes 2097152 | tf_op jit(solution)/shard_map/all_to_all | solution.py:47
  44.9 89.7 %all-reduce.2.cloned.1.call-start = ((), (), s32[]{:S(2)}) async-start(), calls=%async_computation.4 | async-start | bytes 262144 | tf_op jit(solution)/shard_map/psum | solution.py:33
  101.6 75.4 %all-gather.2.cloned.1.call-start = ((), (), s32[]{:S(2)}) async-start(), calls=%async_computation.5 | async-start | bytes 1179648 | tf_op jit(solution)/shard_map/all_gather | solution.py:34
  142.0 37.3 %copy-start.4 = (f32[2048,128]{1,0:T(8,128)}, f32[2048,128]{1,0:T(8,128)S(1)}, u32[]{:S(2)}) copy-start(f32[2048,128]{1,0:T(8,128)S(1)} %get-tuple-element.57) | copy-start | bytes 3145732
Sparse Core Ops, SparseCore 0:
  26.9 74.6 reduce-scatter.1
  103.9 30.6 all-reduce.1
  136.7 40.2 all-gather.1
where the time goes:
time: 186 us
  waiting for transfers between devices  130 us (70%)
  matrix products  24.7 us (13%)
  between operations  13.9 us (7%)
  starting transfers between devices  11 us (6%)
  other arithmetic  3.89 us (2%)
  local copies, waits for them, and re-layouts  2.47 us (1%)
    reduce_scatter x1, waiting for transfers between devices, hot_part(): shared = lax.psum_scatter(local_sum, 'gy', scatter_dimension=0, tiled=True)  56.6 us
    all_gather x1, waiting for transfers between devices, hot_part(): total = lax.all_gather(shared, 'gy', axis=0, tiled=True)  35 us
    psum x1, waiting for transfers between devices, hot_part(): shared = lax.psum(shared, 'gx')  32.9 us
    dot_general x8, matrix products, add_block(): jnp.dot(selector, data_here, preferred_element_type=jnp.float32)  24.7 us
    all_to_all x1, starting transfers between devices, cold_part(): lax.all_to_all(slots_here, 'gy', split_axis=0, concat_axis=0, tiled=True)  7.31 us
    all_to_all x1, waiting for transfers between devices, cold_part(): lax.all_to_all(slots_here, 'gy', split_axis=0, concat_axis=0, tiled=True)  5.07 us
  transfers between devices with their start and end apart: 5, of which 4 were waited for; matrix products, arithmetic and copies ran while one was open for 5% of the time, Pallas kernels for 0%

commit v1 on v0

--- a/solution.py
+++ b/solution.py
@@ -6,6 +6,16 @@
 
 HOT = 2048
 OWN_ROWS = 2048
+
+
+def pass_along(shard, axis, dim):
+    peers = lax.axis_size(axis)
+    block, blocks = (shard, [shard])
+    for _ in range(peers - 1):
+        block = lax.ppermute(block, axis, [(i, (i + 1) % peers) for i in range(peers)])
+        blocks.insert(0, block)
+    row_of_blocks = jnp.concatenate(blocks, axis=dim)
+    return jnp.roll(row_of_blocks, (lax.axis_index(axis) + 1) * shard.shape[dim], axis=dim)
 
 
 def onehot_sum(row_ids, row_data, table_size, block_rows):
@@ -31,7 +41,7 @@
     factor = (hot_rows / (hot_ids.shape[0] * lax.axis_size("gx") * lax.axis_size("gy"))) ** 0.5
     shared = lax.psum_scatter(local_sum, "gy", scatter_dimension=0, tiled=True)
     shared = lax.psum(shared, "gx")
-    total = lax.all_gather(shared, "gy", axis=0, tiled=True)
+    total = pass_along(shared, "gy", 0)
     return total * factor
 
 

time: 186 us -> 199 us (1.070)
  waiting for transfers between devices: 130 us -> 141 us
    ppermute x0 -> x7, waiting for transfers between devices: none -> 46.7 us  [pass_along(): lax.ppermute(block, axis, [(i, (i + 1) % peers) for i in range(peers)])]
    all_gather x1 -> x0, waiting for transfers between devices: 35 us -> none  [hot_part(): total = lax.all_gather(shared, 'gy', axis=0, tiled=True)]
  transfers between devices with their start and end apart: 5 -> 11, of which waited for: 4 -> 10; matrix products, arithmetic and copies ran while one was open for 5% -> 4% of each run, Pallas kernels for 0% -> 0%
where the time goes in v1:
time: 199 us
  waiting for transfers between devices  141 us (71%)
  matrix products  24.7 us (12%)
  between operations  14.3 us (7%)
  starting transfers between devices  12.4 us (6%)
  local copies, waits for them, and re-layouts  2.97 us (1%)
  other arithmetic  2.66 us (1%)
    reduce_scatter x1, waiting for transfers between devices, hot_part(): shared = lax.psum_scatter(local_sum, 'gy', scatter_dimension=0, tiled=True)  56.6 us
    ppermute x7, waiting for transfers between devices, pass_along(): lax.ppermute(block, axis, [(i, (i + 1) % peers) for i in range(peers)])  46.7 us
    psum x1, waiting for transfers between devices, hot_part(): shared = lax.psum(shared, 'gx')  33 us
    dot_general x8, matrix products, add_block(): jnp.dot(selector, data_here, preferred_element_type=jnp.float32)  24.7 us
    all_to_all x1, starting transfers between devices, cold_part(): lax.all_to_all(slots_here, 'gy', split_axis=0, concat_axis=0, tiled=True)  7.31 us
    all_to_all x1, waiting for transfers between devices, cold_part(): lax.all_to_all(slots_here, 'gy', split_axis=0, concat_axis=0, tiled=True)  5.07 us
  transfers between devices with their start and end apart: 11, of which 10 were waited for; matrix products, arithmetic and copies ran while one was open for 4% of the time, Pallas kernels for 0%

profile of v1, /device:TPU:0, one launch (start us, length us, event | category | flops | bytes accessed | tf_op | source)
XLA Modules:
  0.0 198.7 jit_solution(11154275508790630177)
XLA Ops:
  7.2 0.0 reduce-scatter.2.cloned.1.call-start
  7.2 0.8 reshape.43
  8.0 0.0 copy-start.3
  8.0 0.0 copy-start.4
  8.0 0.0 copy-start
  8.0 17.7 %while.22 = (s32[]{:T(128)}, f32[2048,128]{1,0:T(8,128)S(1)}, s32[4,2048]{1,0:T(4,128)S(1)}, bf16[4,2048,128]{2,1,0:T(8,128)(2,1)}, s32[]{:T(128)}, /*index=5*/s32[]{:T(128)}) while((s32[]{:T(128)}, f32[2048,128]{1,0:T(8,128)S(1)}, s32[4,2048]{1,0:T(4,128)S(1)}, bf16[4,2048,128]{2,1,0:T(8,128)(2,1)}, s32[]{:T(128)}, ...), condition=%wide.region_1.2_spmd.clone, body=%wide.region_0.1_spmd.clone.sunk | while | flops 1078460416 | bytes 2646611 | solution.py:33
  8.1 4.4 %fusion.21 = f32[2048,128]{1,0:T(8,128)S(1)} fusion(s32[2048]{0:T(1024)S(1)} %bitcast.25, f32[2048,128]{1,0:T(8,128)S(1)} %get-tuple-element.165, bf16[4,2048,128]{2,1,0:T(8,128)(2,1)} %get-tuple-element.173, s32[]{:T(128)} %get-tuple-element.164, pred[]{:T(512)S(6)} %compare.7), kind=kOutput, calls=%fused_computation.5.clone.1 | convolution fusion | flops 1078460416 | bytes 2630145 | tf_op jit(solution)/shard_map/while/body/eval_jaxpr/dot_general | solution.py:30
  12.6 4.4 %fusion.21 = f32[2048,128]{1,0:T(8,128)S(1)} fusion(s32[2048]{0:T(1024)S(1)} %bitcast.25, f32[2048,128]{1,0:T(8,128)S(1)} %get-tuple-element.165, bf16[4,2048,128]{2,1,0:T(8,128)(2,1)} %get-tuple-element.173, s32[]{:T(128)} %get-tuple-element.164, pred[]{:T(512)S(6)} %compare.7), kind=kOutput, calls=%fused_computation.5.clone.1 | convolution fusion | flops 1078460416 | bytes 2630145 | tf_op jit(solution)/shard_map/while/body/eval_jaxpr/dot_general | solution.py:30
  17.0 4.4 %fusion.21 = f32[2048,128]{1,0:T(8,128)S(1)} fusion(s32[2048]{0:T(1024)S(1)} %bitcast.25, f32[2048,128]{1,0:T(8,128)S(1)} %get-tuple-element.165, bf16[4,2048,128]{2,1,0:T(8,128)(2,1)} %get-tuple-element.173, s32[]{:T(128)} %get-tuple-element.164, pred[]{:T(512)S(6)} %compare.7), kind=kOutput, calls=%fused_computation.5.clone.1 | convolution fusion | flops 1078460416 | bytes 2630145 | tf_op jit(solution)/shard_map/while/body/eval_jaxpr/dot_general | solution.py:30
  21.4 4.4 %fusion.21 = f32[2048,128]{1,0:T(8,128)S(1)} fusion(s32[2048]{0:T(1024)S(1)} %bitcast.25, f32[2048,128]{1,0:T(8,128)S(1)} %get-tuple-element.165, bf16[4,2048,128]{2,1,0:T(8,128)(2,1)} %get-tuple-element.173, s32[]{:T(128)} %get-tuple-element.164, pred[]{:T(512)S(6)} %compare.7), kind=kOutput, calls=%fused_computation.5.clone.1 | convolution fusion | flops 1078460416 | bytes 2630145 | tf_op jit(solution)/shard_map/while/body/eval_jaxpr/dot_general | solution.py:30
  25.7 0.0 copy-start.1
  25.8 1.0 copy-done.1
  26.7 0.0 reduce-scatter.2.cloned.1.call-update
  26.7 0.0 copy-done.3
  26.8 0.6 all_to_all.9
  27.4 7.3 %all-to-all-start = ((s32[8,1,512]{2,1,0:T(1,128)}), s32[8,1,512]{2,1,0:T(1,128)S(1)}, u32[]{:S(2)}, u32[]{:S(2)}) async-start(s32[8,1,512]{2,1,0:T(1,128)} %all_to_all.9), calls=%async_computation.1 | async-start | bytes 32768 | tf_op jit(solution)/shard_map/all_to_all | solution.py:58
  34.7 0.0 copy-done.4
  34.7 0.1 iota_compare_fusion.8
  34.7 0.0 copy-done
  34.8 1.5 bitcast_select_fusion
  36.2 5.1 %all-to-all-done = s32[8,1,512]{2,1,0:T(1,128)S(1)} async-done(((s32[8,1,512]{2,1,0:T(1,128)}), s32[8,1,512]{2,1,0:T(1,128)S(1)}, u32[]{:S(2)}, u32[]{:S(2)}) %all-to-all-start) | async-done | bytes 16416 | tf_op jit(solution)/shard_map/all_to_all | solution.py:58
  41.3 3.6 %all-to-all-start.1 = ((bf16[8,512,128]{2,1,0:T(8,128)(2,1)}), bf16[8,512,128]{2,1,0:T(8,128)(2,1)S(1)}, u32[]{:S(2)}, u32[]{:S(2)}) async-start(bf16[8,512,128]{2,1,0:T(8,128)(2,1)} %bitcast_select_fusion), calls=%async_computation.2 | async-start | bytes 2097152 | tf_op jit(solution)/shard_map/all_to_all | solution.py:57
  44.9 0.0 all-reduce.2.cloned.1.call-start
  44.9 56.6 %reduce-scatter.2.cloned.1.call-done = f32[256,128]{1,0:T(8,128)} async-done(((f32[2048,128]{1,0:T(8,128)}), f32[256,128]{1,0:T(8,128)}) %reduce-scatter.2.cloned.1.call-update) | async-done | bytes 131088 | tf_op jit(solution)/shard_map/reduce_scatter | solution.py:42
  101.5 0.0 all-reduce.2.cloned.1.call-update
  101.6 33.0 %all-reduce.2.cloned.1.call-done = f32[256,128]{1,0:T(8,128)} async-done(((f32[256,128]{1,0:T(8,128)}), f32[256,128]{1,0:T(8,128)}) %all-reduce.2.cloned.1.call-update) | async-done | bytes 131088 | tf_op jit(solution)/shard_map/psum | solution.py:43
  134.6 1.5 collective-permute-start
  136.0 6.4 %collective-permute-done = f32[256,128]{1,0:T(8,128)S(1)} collective-permute-done((f32[256,128]{1,0:T(8,128)}, f32[256,128]{1,0:T(8,128)S(1)}, u32[]{:S(2)}, u32[]{:S(2)}) %collective-permute-start) | collective-permute-done | bytes 131104 | tf_op jit(solution)/shard_map/ppermute | solution.py:15
  142.4 0.0 collective-permute-start.1
  142.4 7.7 %collective-permute-done.1 = f32[256,128]{1,0:T(8,128)S(1)} collective-permute-done((f32[256,128]{1,0:T(8,128)S(1)}, f32[256,128]{1,0:T(8,128)S(1)}, u32[]{:S(2)}, u32[]{:S(2)}) %collective-permute-start.1) | collective-permute-done | bytes 131104 | tf_op jit(solution)/shard_map/ppermute | solution.py:15
  150.1 0.0 collective-permute-start.2
  150.1 7.7 %collective-permute-done.2 = f32[256,128]{1,0:T(8,128)S(1)} collective-permute-done((f32[256,128]{1,0:T(8,128)S(1)}, f32[256,128]{1,0:T(8,128)S(1)}, u32[]{:S(2)}, u32[]{:S(2)}) %collective-permute-start.2) | collective-permute-done | bytes 131104 | tf_op jit(solution)/shard_map/ppermute | solution.py:15
  157.8 0.0 collective-permute-start.3
  157.8 8.4 %collective-permute-done.3 = f32[256,128]{1,0:T(8,128)S(1)} collective-permute-done((f32[256,128]{1,0:T(8,128)S(1)}, f32[256,128]{1,0:T(8,128)S(1)}, u32[]{:S(2)}, u32[]{:S(2)}) %collective-permute-start.3) | collective-permute-done | bytes 131104 | tf_op jit(solution)/shard_map/ppermute | solution.py:15
  166.2 0.0 collective-permute-start.4
  166.2 8.6 %collective-permute-done.4 = f32[256,128]{1,0:T(8,128)S(1)} collective-permute-done((f32[256,128]{1,0:T(8,128)S(1)}, f32[256,128]{1,0:T(8,128)S(1)}, u32[]{:S(2)}, u32[]{:S(2)}) %collective-permute-start.4) | collective-permute-done | bytes 131104 | tf_op jit(solution)/shard_map/ppermute | solution.py:15
  174.8 0.0 collective-permute-start.5
  174.8 7.7 %collective-permute-done.5 = f32[256,128]{1,0:T(8,128)S(1)} collective-permute-done((f32[256,128]{1,0:T(8,128)S(1)}, f32[256,128]{1,0:T(8,128)S(1)}, u32[]{:S(2)}, u32[]{:S(2)}) %collective-permute-start.5) | collective-permute-done | bytes 131104 | tf_op jit(solution)/shard_map/ppermute | solution.py:15
  182.5 0.0 collective-permute-start.6
  182.5 0.0 all-to-all-done.1
  182.5 0.0 copy-start.2
  182.5 7.3 %while.23 = (s32[]{:T(128)}, f32[2048,128]{1,0:T(8,128)S(1)}, s32[4,1024]{1,0:T(4,128)S(1)}, bf16[4,1024,128]{2,1,0:T(8,128)(2,1)S(1)}, s32[]{:T(128)}, /*index=5*/s32[]{:T(128)}) while((s32[]{:T(128)}, f32[2048,128]{1,0:T(8,128)S(1)}, s32[4,1024]{1,0:T(4,128)S(1)}, bf16[4,1024,128]{2,1,0:T(8,128)(2,1)S(1)}, s32[]{:T(128)}, ...), condition=%wide.region_5.6_spmd.clone, body=%wide.region_4.5_spmd.clone.sunk | while | flops 539492352 | bytes 2371671 | solution.py:33
  182.5 1.8 fusion.23
  184.4 1.8 fusion.23
  186.2 1.8 fusion.23
  188.0 1.8 fusion.23
  189.8 0.0 copy-start.5
  189.8 0.3 collective-permute-done.6
  190.3 0.0 copy-done.2
  190.5 0.3 copy-done.5
  190.8 1.1 dynamic-slice_multiply_fusion
  (28 shorter events, 0.3 us)
Async XLA Ops:
  7.2 94.4 %reduce-scatter.2.cloned.1.call-start = ((), (), s32[]{:S(2)}) async-start(), calls=%async_computation.3 | async-start | bytes 1179648 | tf_op jit(solution)/shard_map/reduce_scatter | solution.py:42
  8.0 18.7 %copy-start.3 = (s32[1,1,8,512]{3,2,1,0:T(8,128)S(1)}, s32[1,1,8,512]{3,2,1,0:T(8,128)}, u32[]{:S(2)}) copy-start(s32[1,1,8,512]{3,2,1,0:T(8,128)} %param.12) | copy-start | bytes 49156
  8.0 26.7 %copy-start.4 = (s32[1,1,8]{2,1,0:T(1,128)S(1)}, s32[1,1,8]{2,1,0:T(1,128)}, u32[]{:S(2)}) copy-start(s32[1,1,8]{2,1,0:T(1,128)} %param.13) | copy-start | bytes 100
  8.0 26.7 %copy-start = (bf16[1,1,8,512,128]{4,3,2,1,0:T(8,128)(2,1)S(1)}, bf16[1,1,8,512,128]{4,3,2,1,0:T(8,128)(2,1)}, u32[]{:S(2)}) copy-start(bf16[1,1,8,512,128]{4,3,2,1,0:T(8,128)(2,1)} %param.11) | copy-start | bytes 3145732
  25.7 1.0 copy-start.1
  27.4 13.9 %all-to-all-start = ((s32[8,1,512]{2,1,0:T(1,128)}), s32[8,1,512]{2,1,0:T(1,128)S(1)}, u32[]{:S(2)}, u32[]{:S(2)}) async-start(s32[8,1,512]{2,1,0:T(1,128)} %all_to_all.9), calls=%async_computation.1 | async-start | bytes 32768 | tf_op jit(solution)/shard_map/all_to_all | solution.py:58
  41.3 141.2 %all-to-all-start.1 = ((bf16[8,512,128]{2,1,0:T(8,128)(2,1)}), bf16[8,512,128]{2,1,0:T(8,128)(2,1)S(1)}, u32[]{:S(2)}, u32[]{:S(2)}) async-start(bf16[8,512,128]{2,1,0:T(8,128)(2,1)} %bitcast_select_fusion), calls=%async_computation.2 | async-start | bytes 2097152 | tf_op jit(solution)/shard_map/all_to_all | solution.py:57
  44.9 89.7 %all-reduce.2.cloned.1.call-start = ((), (), s32[]{:S(2)}) async-start(), calls=%async_computation.4 | async-start | bytes 262144 | tf_op jit(solution)/shard_map/psum | solution.py:43
  134.6 7.9 %collective-permute-start = (f32[256,128]{1,0:T(8,128)}, f32[256,128]{1,0:T(8,128)S(1)}, u32[]{:S(2)}, u32[]{:S(2)}) collective-permute-start(f32[256,128]{1,0:T(8,128)} %all-reduce.2.cloned.1.call-done), channel_id=1, source_target_pairs={{0,1},{1,2},{2,3},{3,4},{4,5},{5,6},{6,7},{7,0},{8,9},{9,10},{10,1... | collective-permute-start | bytes 393224 | tf_op jit(solution)/shard_map/ppermute | solution.py:15
  142.4 7.7 %collective-permute-start.1 = (f32[256,128]{1,0:T(8,128)S(1)}, f32[256,128]{1,0:T(8,128)S(1)}, u32[]{:S(2)}, u32[]{:S(2)}) collective-permute-start(f32[256,128]{1,0:T(8,128)S(1)} %collective-permute-done), channel_id=1, source_target_pairs={{0,1},{1,2},{2,3},{3,4},{4,5},{5,6},{6,7},{7,0},{8,9},{9,10},{10,1... | collective-permute-start | bytes 393224 | tf_op jit(solution)/shard_map/ppermute | solution.py:15
  150.1 7.7 %collective-permute-start.2 = (f32[256,128]{1,0:T(8,128)S(1)}, f32[256,128]{1,0:T(8,128)S(1)}, u32[]{:S(2)}, u32[]{:S(2)}) collective-permute-start(f32[256,128]{1,0:T(8,128)S(1)} %collective-permute-done.1), channel_id=1, source_target_pairs={{0,1},{1,2},{2,3},{3,4},{4,5},{5,6},{6,7},{7,0},{8,9},{9,10},{10,1... | collective-permute-start | bytes 393224 | tf_op jit(solution)/shard_map/ppermute | solution.py:15
  157.8 8.4 %collective-permute-start.3 = (f32[256,128]{1,0:T(8,128)S(1)}, f32[256,128]{1,0:T(8,128)S(1)}, u32[]{:S(2)}, u32[]{:S(2)}) collective-permute-start(f32[256,128]{1,0:T(8,128)S(1)} %collective-permute-done.2), channel_id=1, source_target_pairs={{0,1},{1,2},{2,3},{3,4},{4,5},{5,6},{6,7},{7,0},{8,9},{9,10},{10,1... | collective-permute-start | bytes 393224 | tf_op jit(solution)/shard_map/ppermute | solution.py:15
  166.2 8.6 %collective-permute-start.4 = (f32[256,128]{1,0:T(8,128)S(1)}, f32[256,128]{1,0:T(8,128)S(1)}, u32[]{:S(2)}, u32[]{:S(2)}) collective-permute-start(f32[256,128]{1,0:T(8,128)S(1)} %collective-permute-done.3), channel_id=1, source_target_pairs={{0,1},{1,2},{2,3},{3,4},{4,5},{5,6},{6,7},{7,0},{8,9},{9,10},{10,1... | collective-permute-start | bytes 393224 | tf_op jit(solution)/shard_map/ppermute | solution.py:15
  174.8 7.7 %collective-permute-start.5 = (f32[256,128]{1,0:T(8,128)S(1)}, f32[256,128]{1,0:T(8,128)S(1)}, u32[]{:S(2)}, u32[]{:S(2)}) collective-permute-start(f32[256,128]{1,0:T(8,128)S(1)} %collective-permute-done.4), channel_id=1, source_target_pairs={{0,1},{1,2},{2,3},{3,4},{4,5},{5,6},{6,7},{7,0},{8,9},{9,10},{10,1... | collective-permute-start | bytes 393224 | tf_op jit(solution)/shard_map/ppermute | solution.py:15
  182.5 7.7 %collective-permute-start.6 = (f32[256,128]{1,0:T(8,128)S(1)}, f32[256,128]{1,0:T(8,128)S(1)}, u32[]{:S(2)}, u32[]{:S(2)}) collective-permute-start(f32[256,128]{1,0:T(8,128)S(1)} %collective-permute-done.5), channel_id=1, source_target_pairs={{0,1},{1,2},{2,3},{3,4},{4,5},{5,6},{6,7},{7,0},{8,9},{9,10},{10,1... | collective-permute-start | bytes 393224 | tf_op jit(solution)/shard_map/ppermute | solution.py:15
  182.5 7.8 %copy-start.2 = (f32[256,128]{1,0:T(8,128)S(1)}, f32[256,128]{1,0:T(8,128)}, u32[]{:S(2)}) copy-start(f32[256,128]{1,0:T(8,128)} %all-reduce.2.cloned.1.call-done) | copy-start | bytes 393220
  189.8 1.0 copy-start.5
Sparse Core Ops, SparseCore 0:
  26.9 74.6 reduce-scatter.1
  103.9 30.6 all-reduce.1
